TPU v7x, 32 devices: a whole 2x2x4 slice. The times are simulated.
32 devices in a mesh: rep: 4 (over y, x), tile: 8 (over z, core).
Axes of the slice: x: 2, y: 2, z: 4, core: 2. Of those that a mesh axis runs over, the one named last changes fastest.
Arguments:
- spins_in: float32 [4, 2048, 4096], P('rep', 'tile'), may hold values from -1 to 1
- noise: bfloat16 [2, 4, 2048, 4096], P(None, 'rep', 'tile'), may hold values from -1.5 to 1.5
- betas: float32 [4], replicated, as said below
- labels: int32 [4], P('rep'), may hold values from 0 to 3, each once
- accept: int32 [2, 4], P(None, 'rep'), may hold values 0 or 1
Outputs:
- spins: float32 [4, 2048, 4096], P('rep', 'tile')
- energy_rows: float32 [4, 2048], P('rep', 'tile')
- margin_rows: float32 [4, 2048], P('rep', 'tile')
- new_labels: int32 [4], P('rep')
- log_ratio: float32 [4], P('rep')
- new_beta: float32 [4], P('rep')
Inputs may be any that keep to these rules, and one draw needn't show every extreme that they name: `labels`: a permutation of the temperature indices. `accept`: entry [p, r] is read only where r mod 2 equals p. `betas`: distinct and positive.
All inputs are finite; a program needn't handle non-finite values. No bound on the sum of `accept` on one device may be relied on, other than what follows from the above.
Results may differ from a plain program's by a relative error of at most 0.0003.
Values sent between devices are 32-bit elements; how exact they have to be, the bound alone decides.
A program may use at most 64 MiB of HBM per device.

v0:
```python
import functools

import jax
import jax.numpy as jnp
from jax import lax
from jax.experimental import pallas as pl
from jax.experimental.pallas import tpu as pltpu
from jax.sharding import PartitionSpec as P

SWEEPS = 2
STAGES = 2 * SWEEPS
H = 8
LANES = 128
ROWS = 2 * H
PAD = H
EARLY = 9
VMEM_BYTES = 60 * 1024 * 1024
MESH = pl.DeviceIdType.MESH


def kernel(
    n, peers, total_rows,
    spins_ref, noise_ref, betas_hbm, labels_hbm, accept_hbm,
    X, energy_ref, margin_ref, small_ref,
    SI, NB, NF, Q, R, EP, MP, MS, MR, EM, EG, LM, LG, betas_ref, labels_ref, accept_ref,
    s_sem, n_sem, hs_sem, hr_sem, bs_sem, br_sem,
    ms_sem, mr_sem, es_sem, er_sem, ls_sem, lr_sem, i_sem,
):
    T, C = spins_ref.shape[:2]
    rows, cols = T * H, C * LANES
    blocks = rows // ROWS
    half = C // 2
    me = lax.axis_index("rep")
    tile = lax.axis_index("tile")
    nxt = lax.rem(tile + 1, peers)
    prv = lax.rem(tile + peers - 1, peers)
    odd = lax.rem(me, 2)
    near = lax.rem(me + 1 + (n - 2) * odd, n)
    far = lax.rem(me + 2 + (n - 4) * odd, n)

    def load_spins(t):
        return pltpu.make_async_copy(
            spins_ref.at[t], SI.at[:, pl.ds(pl.multiple_of(PAD + t * H, H), H)], s_sem.at[t]
        )

    def load_noise(w, t):
        return pltpu.make_async_copy(noise_ref.at[w, t], NB.at[w, t], n_sem.at[w, t])

    def loaded(t):
        load_spins(t).wait()
        for w in range(SWEEPS):
            load_noise(w, t).wait()

    barrier = pltpu.get_barrier_semaphore()

    @pl.loop(1, peers)
    def _(d):
        pl.semaphore_signal(barrier, inc=1, device_id={"tile": lax.rem(tile + d, peers)}, device_id_type=MESH)

    @pl.loop(1, n)
    def _(d):
        pl.semaphore_signal(barrier, inc=1, device_id={"rep": lax.rem(me + d, n)}, device_id_type=MESH)

    small = [
        pltpu.make_async_copy(src, dst, i_sem.at[k])
        for k, (src, dst) in enumerate(
            ((betas_hbm, betas_ref), (labels_hbm, labels_ref), (accept_hbm, accept_ref))
        )
    ]
    for copy in small:
        copy.start()

    @pl.loop(0, T)
    def _(t):
        load_spins(t).start()
        for w in range(SWEEPS):
            load_noise(w, t).start()

    for copy in small:
        copy.wait()
    beta = jnp.float32(0.0)
    for k in range(n):
        beta = beta + jnp.where(labels_ref[0, 0] == k, betas_ref[k], 0.0)

    def halo_copies():
        copies = []
        for side, (start, slot, dev) in enumerate(((rows, 0, nxt), (PAD, PAD + rows, prv))):
            pairs = [(SI.at[:, pl.ds(start, H)], SI.at[:, pl.ds(slot, H)])]
            pairs += [(NF.at[w, :, pl.ds(start, H)], NF.at[w, :, pl.ds(slot, H)]) for w in range(SWEEPS)]
            for k, (src, dst) in enumerate(pairs):
                copies.append(
                    pltpu.make_async_remote_copy(
                        src, dst, hs_sem.at[side, k], hr_sem.at[side, k],
                        device_id={"tile": dev}, device_id_type=MESH,
                    )
                )
        return copies

    halos = halo_copies()

    def bulk(q, b):
        dest = lax.rem(me + (n - 2 + odd if q == 0 else 1 + odd), n)
        slot = 1 - odd if q == 0 else odd
        where = pl.ds(pl.multiple_of(b * ROWS, ROWS), ROWS)
        return pltpu.make_async_remote_copy(
            X.at[q * half : (q + 1) * half, where], R.at[slot, :, where],
            bs_sem.at[q, b], br_sem.at[slot, b],
            device_id={"rep": dest}, device_id_type=MESH,
        )

    def send(b):
        for q in range(2):
            bulk(q, b).start()

    def bulk_from(slot, b):
        where = pl.ds(pl.multiple_of(b * ROWS, ROWS), ROWS)
        return pltpu.make_async_remote_copy(
            X.at[0:half, where], R.at[slot, :, where], bs_sem.at[0, b], br_sem.at[slot, b],
            device_id={"rep": near}, device_id_type=MESH,
        )

    lane = lax.broadcasted_iota(jnp.int32, (H, LANES), 1)
    even = lax.rem(lane, 2) == 0
    first = lane == 0
    last = lane == LANES - 1

    def convert(t):
        where = pl.ds(pl.multiple_of(PAD + t * H, H), H)
        for w in range(SWEEPS):
            for c in range(C):
                NF[w, c, where, :] = NB[w, t, c].astype(jnp.float32)

    def strided(ref, index, start):
        return ref[(*index, pl.ds(start, H, stride=2), slice(None))]

    def stage(k, p):
        sweep, colour = k // 2, k % 2
        row = PAD + 2 * p

        def centre(c):
            if k:
                return Q[k - 1, c, pl.ds(PAD + p, H), :]
            return jnp.where(even, strided(SI, (c,), row + 1), strided(SI, (c,), row))

        def vertical(c):
            if k:
                before = Q[k - 1, c, pl.ds(PAD + p - 1, H), :]
                after = Q[k - 1, c, pl.ds(PAD + p + 1, H), :]
                return jnp.where(even, before, after) if colour == 0 else jnp.where(even, after, before)
            return jnp.where(even, strided(SI, (c,), row - 1), strided(SI, (c,), row + 2))

        def noise(c):
            upper, lower = strided(NF, (sweep, c), row), strided(NF, (sweep, c), row + 1)
            return jnp.where(even, upper, lower) if colour == 0 else jnp.where(even, lower, upper)

        here = centre(0)
        to_right = pltpu.roll(centre(C - 1), 1, 1)
        to_left = pltpu.roll(here, LANES - 1, 1)
        wrap = to_left
        for c in range(C):
            ahead = centre(c + 1) if c + 1 < C else None
            ahead_left = pltpu.roll(ahead, LANES - 1, 1) if c + 1 < C else wrap
            here_right = pltpu.roll(here, 1, 1)
            left = jnp.where(first, to_right, here_right)
            right = jnp.where(last, ahead_left, to_left)
            field = (here + vertical(c)) + (left + right)
            Q[k, c, pl.ds(PAD + p, H), :] = jnp.tanh(beta * field + noise(c))
            here, to_right, to_left = ahead, here_right, ahead_left

    def finish(b):
        p = pl.multiple_of(PAD + b * H, H)
        row = pl.multiple_of(b * ROWS, ROWS)
        for c in range(C):
            e, o = Q[2, c, pl.ds(p, H), :], Q[3, c, pl.ds(p, H), :]
            X[c, pl.ds(row, H, stride=2), :] = jnp.where(even, e, o)
            X[c, pl.ds(row + 1, H, stride=2), :] = jnp.where(even, o, e)

    def bonds(b):
        p = pl.multiple_of(PAD + b * H, H)
        row = pl.multiple_of(b * ROWS, ROWS)

        def pair(c):
            e, o = Q[2, c, pl.ds(p, H), :], Q[3, c, pl.ds(p, H), :]
            upper, lower = jnp.where(even, e, o), jnp.where(even, o, e)
            return upper, lower, pltpu.roll(upper, LANES - 1, 1), pltpu.roll(lower, LANES - 1, 1)

        here = pair(0)
        wrap = here
        total_upper = jnp.zeros((H, LANES), jnp.float32)
        total_lower = jnp.zeros((H, LANES), jnp.float32)
        for c in range(C):
            ahead = pair(c + 1) if c + 1 < C else wrap
            upper, lower, upper_left, lower_left = here
            below = jnp.where(even, Q[2, c, pl.ds(p + 1, H), :], Q[3, c, pl.ds(p + 1, H), :])
            total_upper = total_upper + upper * (lower + jnp.where(last, ahead[2], upper_left))
            total_lower = total_lower + lower * (below + jnp.where(last, ahead[3], lower_left))
            here = ahead
        EP[pl.ds(row, H, stride=2), :] = total_upper
        EP[pl.ds(row + 1, H, stride=2), :] = total_lower

    for t in range(4):
        loaded(t)
    convert(0)

    @pl.loop(0, blocks + 1)
    def _(s):
        final = s // blocks
        middle = 1 - final

        @pl.when((s >= 1) & (s < 3))
        def _():
            loaded(2 * s + 2)
            loaded(2 * s + 3)

        @pl.when(s == 3)
        def _():
            @pl.loop(8, T)
            def _(t):
                loaded(t)

        @pl.when(s < blocks - 1)
        def _():
            convert(2 * s + 1)
            convert(2 * s + 2)

        @pl.when(s == 4)
        def _():
            convert(T - 1)

        @pl.when(s == blocks - 1)
        def _():
            for copy in halos:
                copy.wait_recv()

        for k in range(STAGES):
            stage(k, middle * (s * H + STAGES - k) + final * (k - STAGES + 1))

        @pl.when(s == 1)
        def _():
            pl.semaphore_wait(barrier, n - 1 + peers - 1)

        @pl.when(s >= 1)
        def _():
            b = middle * s
            finish(b)
            bonds(b)

            @pl.when(s <= EARLY)
            def _():
                send(b)

        @pl.when(s == 4)
        def _():
            for copy in halos:
                copy.start()

    per_row = jnp.sum(EP[...].T, axis=0, keepdims=True) * (-1.0 / cols)
    energy_ref[...] = per_row
    local = jnp.broadcast_to(jnp.sum(per_row, axis=1, keepdims=True), (8, LANES))
    EM[...] = local
    EG[tile] = local

    def energy_copy(d):
        return pltpu.make_async_remote_copy(
            EM, EG.at[tile], es_sem.at[d], er_sem.at[tile],
            device_id={"tile": lax.rem(tile + d, peers)}, device_id_type=MESH,
        )

    def energy_from(d):
        src = lax.rem(tile + d, peers)
        return pltpu.make_async_remote_copy(
            EM, EG.at[src], es_sem.at[d], er_sem.at[src], device_id={"tile": src}, device_id_type=MESH
        )

    @pl.loop(1, peers)
    def _(d):
        energy_copy(d).start()

    @pl.loop(1, peers)
    def _(d):
        energy_from(d).wait_recv()

    energy = jnp.sum(EG[...], axis=0) / total_rows
    line = lax.broadcasted_iota(jnp.int32, (8, LANES), 0)
    label_float = labels_ref[0, 0].astype(jnp.float32)
    accept_zero = accept_ref[0, 0].astype(jnp.float32)
    accept_one = accept_ref[0, 1].astype(jnp.float32)
    message = jnp.where(
        line == 0, energy,
        jnp.where(line == 1, label_float, jnp.where(line == 2, accept_zero, accept_one)),
    )
    LM[...] = message
    LG[me] = message

    def ladder_copy(d):
        return pltpu.make_async_remote_copy(
            LM, LG.at[me], ls_sem.at[d], lr_sem.at[me],
            device_id={"rep": lax.rem(me + d, n)}, device_id_type=MESH,
        )

    def ladder_from(d):
        src = lax.rem(me + d, n)
        return pltpu.make_async_remote_copy(
            LM, LG.at[src], ls_sem.at[d], lr_sem.at[src], device_id={"rep": src}, device_id_type=MESH
        )

    @pl.loop(1, n)
    def _(d):
        ladder_copy(d).start()

    @pl.loop(EARLY + 1, blocks)
    def _(b):
        send(b)

    send(0)

    def margins(b):
        for slot in range(2):
            bulk_from(slot, b).wait_recv()
        for g in range(2):
            where = pl.ds(pl.multiple_of(b * ROWS + g * H, H), H)
            totals = [jnp.zeros((H, LANES), jnp.float32) for _ in range(2)]
            for c in range(half):
                own, one, two = X[odd * half + c, where, :], R[0, c, where, :], R[1, c, where, :]
                totals[0] = totals[0] + own * one
                totals[1] = totals[1] + one * two
            for q in range(2):
                MP[q, where, :] = totals[q]

    def margin_sums(start, stop):
        for q in range(2):
            sums = jnp.sum(MP[q, start:stop, :].T, axis=0, keepdims=True) * (1.0 / cols)
            MS[q, :, start:stop] = jnp.broadcast_to(sums, (8, stop - start))

    @pl.loop(1, blocks // 2)
    def _(b):
        margins(b)

    @pl.loop(1, n)
    def _(d):
        ladder_from(d).wait_recv()

    energies = [LG[r][0:1] for r in range(n)]
    labels = [LG[r][1:2] for r in range(n)]
    acc = [[LG[r][2 + p : 3 + p] for r in range(n)] for p in range(2)]

    def beta_of(label):
        value = jnp.zeros((1, LANES), jnp.float32)
        for k in range(n):
            value = value + jnp.where(label == float(k), betas_ref[k], 0.0)
        return value

    def swapped(current, accepts, start):
        result = list(current)
        for r in range(start, n, 2):
            o = (r + 1) % n
            take = accepts[r] == 1.0
            result[r] = jnp.where(take, current[o], current[r])
            result[o] = jnp.where(take, current[r], current[o])
        return result

    labels_one = swapped(labels, acc[0], 0)
    labels_two = swapped(labels_one, acc[1], 1)
    zero = [beta_of(x) for x in labels]
    one = [beta_of(x) for x in labels_one]
    two = [beta_of(x) for x in labels_two]
    my_label = jnp.zeros((1, LANES), jnp.float32)
    my_log = my_label
    my_beta = my_label
    for r in range(n):
        o = (r + 1) % n
        betas_here = zero if r % 2 == 0 else one
        log = (betas_here[r] - betas_here[o]) * (energies[r] - energies[o])
        my_label = jnp.where(me == r, labels_two[r], my_label)
        my_log = jnp.where(me == r, log, my_log)
        my_beta = jnp.where(me == r, two[r], my_beta)
    small_ref[...] = jnp.concatenate([my_label, my_log, my_beta, jnp.zeros((5, LANES), jnp.float32)], axis=0)

    @pl.loop(blocks // 2, blocks)
    def _(b):
        margins(b)

    margin_sums(rows // 2, rows)
    margins(0)
    margin_sums(0, rows // 2)

    home = pltpu.make_async_remote_copy(
        MS.at[1 - odd], MR.at[0], ms_sem.at[0], mr_sem.at[0], device_id={"rep": near}, device_id_type=MESH
    )
    away = pltpu.make_async_remote_copy(
        MS.at[1], MR.at[1], ms_sem.at[1], mr_sem.at[1], device_id={"rep": far}, device_id_type=MESH
    )
    home.start()

    @pl.when(odd == 1)
    def _():
        away.start()

    for copy in halos:
        copy.wait_send()

    @pl.loop(0, blocks)
    def _(b):
        for q in range(2):
            bulk(q, b).wait_send()

    @pl.loop(1, peers)
    def _(d):
        energy_copy(d).wait_send()

    @pl.loop(1, n)
    def _(d):
        ladder_copy(d).wait_send()

    home.wait()

    @pl.when(odd == 0)
    def _():
        margin_ref[...] = MS[0, 0:1, :] + MR[0, 0:1, :]

    @pl.when(odd == 1)
    def _():
        away.wait()
        margin_ref[...] = MR[0, 0:1, :] + MR[1, 0:1, :]


def settle(spins, energy, margin, small, *refs):
    spins_out, energy_out, margin_out, label_out, log_out, beta_out = refs[:6]
    label, log, beta, sem = refs[6:]
    T = spins_out.shape[0]
    pairs = [(energy, energy_out), (margin, margin_out)]
    pairs += [(spins.at[:, pl.ds(t * H, H)], spins_out.at[t]) for t in range(T)]
    pairs += [(label, label_out), (log, log_out), (beta, beta_out)]
    copies = [pltpu.make_async_copy(a, b, sem.at[k]) for k, (a, b) in enumerate(pairs)]
    for copy in copies[:-3]:
        copy.start()
    label[0] = jnp.max(small[0:1]).astype(jnp.int32)
    log[0] = jnp.max(small[1:2])
    beta[0] = jnp.max(small[2:3])
    for copy in copies[-3:]:
        copy.start()
    for copy in copies:
        copy.wait()


def body(n, peers, total_rows, spins_in, noise, betas, labels, accept):
    _, rows, cols = spins_in.shape
    T, C = rows // H, cols // LANES
    blocks = rows // ROWS
    f32 = jnp.float32
    limit = VMEM_BYTES - 4 * (rows * cols + 2 * rows + 8 * LANES)
    hbm = pl.BlockSpec(memory_space=pltpu.HBM)
    vmem = pl.BlockSpec(memory_space=pltpu.VMEM)
    dma = pltpu.SemaphoreType.DMA
    accept = jnp.transpose(accept)
    labels = labels.reshape(1, 1)
    spins_in = spins_in.reshape(T, H, C, LANES).transpose(0, 2, 1, 3)
    noise = noise.reshape(SWEEPS, T, H, C, LANES).transpose(0, 1, 3, 2, 4)
    results = pl.pallas_call(
        functools.partial(kernel, n, peers, total_rows),
        out_shape=(
            pltpu.VMEM((C, rows, LANES), f32),
            pltpu.VMEM((1, rows), f32),
            pltpu.VMEM((1, rows), f32),
            pltpu.VMEM((8, LANES), f32),
        ),
        in_specs=[hbm] * 5,
        out_specs=(vmem,) * 4,
        scratch_shapes=[
            pltpu.VMEM((C, rows + 3 * PAD, LANES), f32),
            pltpu.VMEM((SWEEPS, T, C, H, LANES), jnp.bfloat16),
            pltpu.VMEM((SWEEPS, C, rows + 3 * PAD, LANES), f32),
            pltpu.VMEM((STAGES, C, rows // 2 + 2 * PAD, LANES), f32),
            pltpu.VMEM((2, C // 2, rows, LANES), f32),
            pltpu.VMEM((rows, LANES), f32),
            pltpu.VMEM((2, rows, LANES), f32),
            pltpu.VMEM((2, 8, rows), f32),
            pltpu.VMEM((2, 8, rows), f32),
            pltpu.VMEM((8, LANES), f32),
            pltpu.VMEM((peers, 8, LANES), f32),
            pltpu.VMEM((8, LANES), f32),
            pltpu.VMEM((n, 8, LANES), f32),
            pltpu.SMEM(betas.shape, f32),
            pltpu.SMEM(labels.shape, jnp.int32),
            pltpu.SMEM(accept.shape, jnp.int32),
            dma((T,)),
            dma((SWEEPS, T)),
            dma((2, 1 + SWEEPS)),
            dma((2, 1 + SWEEPS)),
            dma((2, blocks)),
            dma((2, blocks)),
            dma((2,)),
            dma((2,)),
            dma((peers,)),
            dma((peers,)),
            dma((n,)),
            dma((n,)),
            dma((3,)),
        ],
        compiler_params=pltpu.CompilerParams(collective_id=0, has_side_effects=True, vmem_limit_bytes=limit),
        name="lattice_exchange",
    )(spins_in, noise, betas, labels, accept)
    out = pl.pallas_call(
        settle,
        out_shape=(
            jax.ShapeDtypeStruct(spins_in.shape, f32),
            jax.ShapeDtypeStruct((1, rows), f32),
            jax.ShapeDtypeStruct((1, rows), f32),
            jax.ShapeDtypeStruct((1,), jnp.int32),
            jax.ShapeDtypeStruct((1,), f32),
            jax.ShapeDtypeStruct((1,), f32),
        ),
        in_specs=[vmem] * 4,
        out_specs=(hbm,) * 6,
        scratch_shapes=[
            pltpu.SMEM((1,), jnp.int32),
            pltpu.SMEM((1,), f32),
            pltpu.SMEM((1,), f32),
            dma((T + 5,)),
        ],
        compiler_params=pltpu.CompilerParams(vmem_limit_bytes=VMEM_BYTES // 2),
        name="settle",
    )(*results)
    spins = out[0].transpose(0, 2, 1, 3).reshape(1, rows, cols)
    return (spins, *out[1:])


def solution(mesh):
    n = mesh.shape["rep"]
    peers = mesh.shape["tile"]
    in_specs = (P("rep", "tile", None), P(None, "rep", "tile", None), P(), P("rep"), P(None, "rep"))
    out_specs = (P("rep", "tile", None), P("rep", "tile"), P("rep", "tile"), P("rep"), P("rep"), P("rep"))

    def run(spins_in, noise, betas, labels, accept):
        total_rows = spins_in.shape[1]
        step = jax.shard_map(
            functools.partial(body, n, peers, total_rows),
            mesh=mesh, in_specs=in_specs, out_specs=out_specs, check_vma=False,
        )
        return step(spins_in, noise, betas, labels, accept)

    return run
```

profile of v0, /device:TPU:0, one launch (start us, length us, event | category | flops | bytes accessed | tf_op | source)
XLA Modules:
  0.0 61.6 jit_solution(11103386637002897373)
XLA Ops:
  1.3 58.0 %lattice_exchange.1 = (f32[32,256,128]{2,1,0:T(8,128)S(1)}, f32[1,256]{1,0:T(1,128)S(1)}, f32[1,256]{1,0:T(1,128)S(1)}, f32[8,128]{1,0:T(8,128)S(1)}) custom-call(f32[32,32,8,128]{3,2,1,0:T(8,128)} %bitcast.12, bf16[2,32,32,8,128]{4,3,2,1,0:T(8,128)(2,1)} %bitcast.13, f32[4]{0:T(128)} %betas_hbm.1, s32[1,1]{1,0:T(1,128)} %bitcast.11.labels_hbm, s32[1,2]{1,0:T(1,128)} %bitcast.14), custom_call_target="tpu_custom_call" | custom-call | tf_op jit(solution)/shard_map/lattice_exchange/pallas_call | solution.py:459
  59.3 2.3 %settle.1 = (f32[32,32,8,128]{3,2,1,0:T(8,128)}, f32[1,256]{1,0:T(1,128)}, f32[1,256]{1,0:T(1,128)}, s32[1]{0:T(128)}, f32[1]{0:T(128)}, /*index=5*/f32[1]{0:T(128)}) custom-call(f32[32,256,128]{2,1,0:T(8,128)S(1)} %get-tuple-element.16.spins, f32[1,256]{1,0:T(1,128)S(1)} %get-tuple-element.17.energy, f32[1,256]{1,0:T(1,128)S(1)} %get-tuple-element.18.margin, ...), custom_call_target="tpu_custom_call" | custom-call | tf_op jit(solution)/shard_map/settle/pallas_call | solution.py:503
where the time goes:
time: 61.8 us; the launch traced here: 61.6 us
  Pallas kernels  60.3 us (98%)
  between operations  1.29 us (2%)
    pallas_call x1, Pallas kernels, body(): pl.pallas_call(functools.partial(kernel, n, peers, total_rows), out_shape...  58 us
    pallas_call x1, Pallas kernels, body(): pl.pallas_call(settle, out_shape=(jax.ShapeDtypeStruct(spins_in.shape, f3...  2.34 us

commit v1 on v0

v1 whole, which is shorter than its diff:
```python
import functools

import jax
import jax.numpy as jnp
from jax import lax
from jax.experimental import pallas as pl
from jax.experimental.pallas import tpu as pltpu
from jax.sharding import PartitionSpec as P

SWEEPS = 2
STAGES = 2 * SWEEPS
H = 8
LANES = 128
ROWS = 2 * H
PAD = H
EARLY = 9
HALO = 6
PARTS = 4
SOON = 6
GATHER = 4
VMEM_BYTES = 60 * 1024 * 1024
MESH = pl.DeviceIdType.MESH


def kernel(
    n, peers, total_rows,
    spins_ref, noise_ref, betas_hbm, labels_hbm, accept_hbm,
    X, energy_ref, margin_ref, small_ref,
    G, NB, Q0, Q1, Q2, Q3, R, EP, MP, MS, MR, EM, EG, LM, LG, betas_ref, labels_ref, accept_ref,
    s_sem, n_sem, hs_sem, hr_sem, bs_sem, br_sem,
    ms_sem, mr_sem, es_sem, er_sem, ls_sem, lr_sem, i_sem, go_sem,
):
    T, C = spins_ref.shape[:2]
    rows, cols = T * H, C * LANES
    blocks = rows // ROWS
    half = C // 2
    me = lax.axis_index("rep")
    tile = lax.axis_index("tile")
    nxt = lax.rem(tile + 1, peers)
    prv = lax.rem(tile + peers - 1, peers)
    odd = lax.rem(me, 2)
    near = lax.rem(me + 1 + (n - 2) * odd, n)
    far = lax.rem(me + 2 + (n - 4) * odd, n)
    onward = lax.rem(me + n - 2 + 4 * odd, n)

    part = half // PARTS
    member = lax.rem((me + 1) // 2, 2)
    core = lax.rem(tile, 2)
    Q = (Q0, Q1, Q2, Q3)

    def load_spins(t, k):
        return pltpu.make_async_copy(
            spins_ref.at[t], G.at[0, :, pl.ds(pl.multiple_of(PAD + t * H, H), H)], s_sem.at[k]
        )

    def load_noise(w, start, stop, k):
        return pltpu.make_async_copy(noise_ref.at[w, start:stop], NB.at[w, start:stop], n_sem.at[w, k])

    def loaded(start, stop, k):
        pltpu.make_async_copy(spins_ref.at[start:stop], spins_ref.at[start:stop], s_sem.at[k]).wait()
        for w in range(SWEEPS):
            load_noise(w, start, stop, k).wait()

    small = [
        pltpu.make_async_copy(src, dst, i_sem.at[k])
        for k, (src, dst) in enumerate(
            ((betas_hbm, betas_ref), (labels_hbm, labels_ref), (accept_hbm, accept_ref))
        )
    ]
    for copy in small:
        copy.start()

    for w in range(SWEEPS):
        load_noise(w, 0, SOON, 0).start()
    for t in range(SOON):
        load_spins(t, 0).start()

    barrier = pltpu.get_barrier_semaphore()

    @pl.when(member == 1)
    def _():
        for peer in (near, onward):
            pl.semaphore_signal(barrier, inc=1, device_id={"rep": peer}, device_id_type=MESH)

    @pl.loop(1, peers)
    def _(d):
        pl.semaphore_signal(
            barrier, inc=1,
            device_id={"rep": me + (1 - member) * (near - me), "tile": lax.rem(tile + d, peers)}, device_id_type=MESH,
        )

    halos = [
        pltpu.make_async_remote_copy(
            G.at[:, :, pl.ds(start, H)], G.at[:, :, pl.ds(slot, H)], hs_sem.at[side], hr_sem.at[side],
            device_id={"tile": dev}, device_id_type=MESH,
        )
        for side, (start, slot, dev) in enumerate(((rows, 0, nxt), (PAD, PAD + rows, prv)))
    ]

    def bulk(q, b, start, width):
        dest = lax.rem(me + (n - 2 + odd if q == 0 else 1 + odd), n)
        slot = 1 - odd if q == 0 else odd
        where = pl.ds(pl.multiple_of(b * ROWS, ROWS), ROWS)
        group = (b // GATHER) if not isinstance(b, int) or b else blocks // GATHER
        return pltpu.make_async_remote_copy(
            X.at[pl.ds(q * half + start, width), where], R.at[pl.ds(slot * half + start, width), where],
            bs_sem, br_sem.at[group],
            device_id={"rep": dest}, device_id_type=MESH,
        )

    def send(b, start=0, width=half):
        for q in range(2):
            bulk(q, b, start, width).start()

    def gathered(start, stop, group):
        where = slice(start * ROWS, stop * ROWS)
        pltpu.make_async_remote_copy(
            X.at[:, where], R.at[:, where], bs_sem, br_sem.at[group],
            device_id={"rep": near}, device_id_type=MESH,
        ).wait_recv()

    lane = lax.broadcasted_iota(jnp.int32, (H, LANES), 1)
    even = lax.rem(lane, 2) == 0
    first = lane == 0
    last = lane == LANES - 1

    def convert(t, cs=range(C)):
        where = pl.ds(pl.multiple_of(PAD + t * H, H), H)
        for w in range(SWEEPS):
            for c in cs:
                G[1 + w, c, where, :] = NB[w, t, c].astype(jnp.float32)

    def strided(plane, c, start):
        return G[plane, c, pl.ds(start, H, stride=2), :]

    def stage(k, p, cs=range(C), ring=True):
        sweep, colour = k // 2, k % 2
        row = PAD + 2 * p

        def centre(c):
            if k:
                return Q[k - 1][c, pl.ds(PAD + p, H), :]
            return jnp.where(even, strided(0, c, row + 1), strided(0, c, row))

        def vertical(c):
            if k:
                before = Q[k - 1][c, pl.ds(PAD + p - 1, H), :]
                after = Q[k - 1][c, pl.ds(PAD + p + 1, H), :]
                return jnp.where(even, before, after) if colour == 0 else jnp.where(even, after, before)
            return jnp.where(even, strided(0, c, row - 1), strided(0, c, row + 2))

        def noise(c):
            upper, lower = strided(1 + sweep, c, row), strided(1 + sweep, c, row + 1)
            return jnp.where(even, upper, lower) if colour == 0 else jnp.where(even, lower, upper)

        def beside(c, d):
            return (c + d) % C

        count = len(cs)
        here = centre(cs[0])
        to_right = pltpu.roll(centre(cs[-1] if ring else beside(cs[0], -1)), 1, 1)
        to_left = pltpu.roll(here, LANES - 1, 1)
        wrap = to_left if ring else pltpu.roll(centre(beside(cs[-1], 1)), LANES - 1, 1)
        for i, c in enumerate(cs):
            ahead = centre(cs[i + 1]) if i + 1 < count else None
            ahead_left = pltpu.roll(ahead, LANES - 1, 1) if i + 1 < count else wrap
            here_right = pltpu.roll(here, 1, 1)
            left = jnp.where(first, to_right, here_right)
            right = jnp.where(last, ahead_left, to_left)
            field = (here + vertical(c)) + (left + right)
            Q[k][c, pl.ds(PAD + p, H), :] = jnp.tanh(beta * field + noise(c))
            here, to_right, to_left = ahead, here_right, ahead_left

    def finish(b, cs=range(C)):
        p = pl.multiple_of(PAD + b * H, H)
        row = pl.multiple_of(b * ROWS, ROWS)
        for c in cs:
            e, o = Q2[c, pl.ds(p, H), :], Q3[c, pl.ds(p, H), :]
            X[c, pl.ds(row, H, stride=2), :] = jnp.where(even, e, o)
            X[c, pl.ds(row + 1, H, stride=2), :] = jnp.where(even, o, e)

    def bonds(b):
        p = pl.multiple_of(PAD + b * H, H)
        row = pl.multiple_of(b * ROWS, ROWS)

        def pair(c):
            e, o = Q2[c, pl.ds(p, H), :], Q3[c, pl.ds(p, H), :]
            upper, lower = jnp.where(even, e, o), jnp.where(even, o, e)
            return upper, lower, pltpu.roll(upper, LANES - 1, 1), pltpu.roll(lower, LANES - 1, 1)

        here = pair(0)
        wrap = here
        total_upper = jnp.zeros((H, LANES), jnp.float32)
        total_lower = jnp.zeros((H, LANES), jnp.float32)
        for c in range(C):
            ahead = pair(c + 1) if c + 1 < C else wrap
            upper, lower, upper_left, lower_left = here
            below = jnp.where(even, Q2[c, pl.ds(p + 1, H), :], Q3[c, pl.ds(p + 1, H), :])
            total_upper = total_upper + upper * (lower + jnp.where(last, ahead[2], upper_left))
            total_lower = total_lower + lower * (below + jnp.where(last, ahead[3], lower_left))
            here = ahead
        EP[pl.ds(row, H, stride=2), :] = total_upper
        EP[pl.ds(row + 1, H, stride=2), :] = total_lower

    def forward():
        pl.semaphore_wait(barrier, 2)
        for peer in (near, onward):
            pl.semaphore_signal(go_sem.at[0], inc=1, device_id={"rep": peer}, device_id_type=MESH)

    @pl.when(me == n - 1)
    def _():
        forward()

    loaded(0, SOON, 0)

    for w in range(SWEEPS):
        load_noise(w, SOON, T, 1).start()

    @pl.loop(SOON, T)
    def _(t):
        load_spins(t, 1).start()

    for copy in small:
        copy.wait()
    beta = jnp.float32(0.0)
    for k in range(n):
        beta = beta + jnp.where(labels_ref[0, 0] == k, betas_ref[k], 0.0)

    def opening(low, high, index):
        spans = []
        for k in range(STAGES):
            reach = STAGES - 1 - k
            start, stop = low(reach), high(reach)
            spans.append([[(index + q * half + i) % C for i in range(start, stop)] for q in range(2)])
        for cs in spans[0]:
            for t in range(SOON - 1):
                convert(t, cs)
        for k in range(STAGES):
            for cs in spans[k]:
                for s in range(2):
                    stage(k, s * H + STAGES - k, cs, ring=False)
        for q in range(2):
            finish(1, [index + q * half + i for i in range(low(0), high(0))])

    opening(lambda reach: -reach, lambda reach: part + reach, 0)

    @pl.when(me == 0)
    def _():
        forward()

    @pl.when(member == 1)
    def _():
        pl.semaphore_wait(go_sem.at[0], 2)

    send(1, 0, part)
    opening(lambda reach: reach, lambda reach: half - part + reach, part)
    send(1, part, half - part)
    bonds(1)
    loaded(SOON, T, 1)

    @pl.loop(2, blocks + 1)
    def _(s):
        final = s // blocks
        middle = 1 - final

        @pl.when(s < blocks - 1)
        def _():
            convert(2 * s + 1)
            convert(2 * s + 2)

        @pl.when(s == HALO)
        def _():
            convert(T - 1)

            @pl.when(member == 1)
            def _():
                pl.semaphore_wait(barrier, 2 * (peers - 1))
                pl.semaphore_signal(go_sem.at[1], inc=1, device_id={"rep": near}, device_id_type=MESH)

            @pl.when(member == 0)
            def _():
                pl.semaphore_wait(go_sem.at[1], 1)

        @pl.when(s == blocks - 1)
        def _():
            for copy in halos:
                copy.wait_recv()

        for k in range(STAGES):
            stage(k, middle * (s * H + STAGES - k) + final * (k - STAGES + 1))

        b = middle * s
        finish(b)
        bonds(b)

        @pl.when(s <= EARLY)
        def _():
            send(s)

        @pl.when(s == HALO)
        def _():
            for copy in halos:
                copy.start()

    per_row = jnp.sum(EP[...].T, axis=0, keepdims=True) * (-1.0 / cols)
    energy_ref[...] = per_row
    local = jnp.broadcast_to(jnp.sum(per_row, axis=1, keepdims=True), (8, LANES))
    EM[...] = local
    EG[tile] = local

    def energy_copy(d):
        return pltpu.make_async_remote_copy(
            EM, EG.at[tile], es_sem, er_sem,
            device_id={"tile": lax.rem(tile + d, peers)}, device_id_type=MESH,
        )

    others = pltpu.make_async_remote_copy(
        EG.at[: peers - 1], EG.at[: peers - 1], es_sem, er_sem, device_id={"tile": nxt}, device_id_type=MESH
    )

    @pl.loop(1, peers)
    def _(d):
        energy_copy(d).start()

    others.wait_recv()

    energy = jnp.sum(EG[...], axis=0) / total_rows
    line = lax.broadcasted_iota(jnp.int32, (8, LANES), 0)
    label_float = labels_ref[0, 0].astype(jnp.float32)
    accept_zero = accept_ref[0, 0].astype(jnp.float32)
    accept_one = accept_ref[0, 1].astype(jnp.float32)
    message = jnp.where(
        line == 0, energy,
        jnp.where(line == 1, label_float, jnp.where(line == 2, accept_zero, accept_one)),
    )
    LM[...] = message
    LG[me] = message

    def ladder_copy(d):
        return pltpu.make_async_remote_copy(
            LM, LG.at[me], ls_sem, lr_sem,
            device_id={"rep": lax.rem(me + d, n)}, device_id_type=MESH,
        )

    rest = pltpu.make_async_remote_copy(
        LG.at[: n - 1], LG.at[: n - 1], ls_sem, lr_sem, device_id={"rep": near}, device_id_type=MESH
    )

    @pl.loop(1, n)
    def _(d):
        ladder_copy(d).start()

    @pl.loop(EARLY + 1, blocks)
    def _(b):
        send(b)

    @pl.when(core == 0)
    def _():
        send(0)

    def margins(b):
        for g in range(2):
            where = pl.ds(pl.multiple_of(b * ROWS + g * H, H), H)
            totals = [jnp.zeros((H, LANES), jnp.float32) for _ in range(2)]
            for c in range(half):
                own, one, two = X[odd * half + c, where, :], R[c, where, :], R[half + c, where, :]
                totals[0] = totals[0] + own * one
                totals[1] = totals[1] + one * two
            for q in range(2):
                MP[q, where, :] = totals[q]

    def margin_sums(start, stop):
        for q in range(2):
            sums = jnp.sum(MP[q, start:stop, :].T, axis=0, keepdims=True) * (1.0 / cols)
            MS[q, :, start:stop] = jnp.broadcast_to(sums, (8, stop - start))

    def collect(group):
        start, stop = max(1, group * GATHER), (group + 1) * GATHER
        gathered(start, stop, group)

        @pl.loop(start, stop)
        def _(b):
            margins(b)

    groups = blocks // GATHER
    for group in range(groups // 2):
        collect(group)

    rest.wait_recv()

    energies = [LG[r][0:1] for r in range(n)]
    labels = [LG[r][1:2] for r in range(n)]
    acc = [[LG[r][2 + p : 3 + p] for r in range(n)] for p in range(2)]

    def beta_of(label):
        value = jnp.zeros((1, LANES), jnp.float32)
        for k in range(n):
            value = value + jnp.where(label == float(k), betas_ref[k], 0.0)
        return value

    def swapped(current, accepts, start):
        result = list(current)
        for r in range(start, n, 2):
            o = (r + 1) % n
            take = accepts[r] == 1.0
            result[r] = jnp.where(take, current[o], current[r])
            result[o] = jnp.where(take, current[r], current[o])
        return result

    labels_one = swapped(labels, acc[0], 0)
    labels_two = swapped(labels_one, acc[1], 1)
    zero = [beta_of(x) for x in labels]
    one = [beta_of(x) for x in labels_one]
    two = [beta_of(x) for x in labels_two]
    my_label = jnp.zeros((1, LANES), jnp.float32)
    my_log = my_label
    my_beta = my_label
    for r in range(n):
        o = (r + 1) % n
        betas_here = zero if r % 2 == 0 else one
        log = (betas_here[r] - betas_here[o]) * (energies[r] - energies[o])
        my_label = jnp.where(me == r, labels_two[r], my_label)
        my_log = jnp.where(me == r, log, my_log)
        my_beta = jnp.where(me == r, two[r], my_beta)
    small_ref[...] = jnp.concatenate([my_label, my_log, my_beta, jnp.zeros((5, LANES), jnp.float32)], axis=0)

    for group in range(groups // 2, groups):
        collect(group)

    @pl.when(core == 1)
    def _():
        send(0)

    margin_sums(rows // 2, rows)
    gathered(0, 1, groups)
    margins(0)
    margin_sums(0, rows // 2)

    home = pltpu.make_async_remote_copy(
        MS.at[1 - odd], MR.at[0], ms_sem.at[0], mr_sem.at[0], device_id={"rep": near}, device_id_type=MESH
    )
    away = pltpu.make_async_remote_copy(
        MS.at[1], MR.at[1], ms_sem.at[1], mr_sem.at[1], device_id={"rep": far}, device_id_type=MESH
    )
    home.start()

    @pl.when(odd == 1)
    def _():
        away.start()

    for copy in halos:
        copy.wait_send()

    pltpu.make_async_remote_copy(
        X, R, bs_sem, br_sem.at[0], device_id={"rep": near}, device_id_type=MESH
    ).wait_send()
    others.wait_send()
    rest.wait_send()
    home.wait()

    @pl.when(odd == 0)
    def _():
        margin_ref[...] = MS[0, 0:1, :] + MR[0, 0:1, :]

    @pl.when(odd == 1)
    def _():
        away.wait()
        margin_ref[...] = MR[0, 0:1, :] + MR[1, 0:1, :]


def settle(spins, energy, margin, small, *refs):
    spins_out, energy_out, margin_out, label_out, log_out, beta_out = refs[:6]
    label, log, beta, sem = refs[6:]
    T = spins_out.shape[0]
    pairs = [(energy, energy_out), (margin, margin_out)]
    pairs += [(label, label_out), (log, log_out), (beta, beta_out)]
    copies = [pltpu.make_async_copy(a, b, sem.at[k]) for k, (a, b) in enumerate(pairs)]
    for t in range(T):
        pltpu.make_async_copy(spins.at[:, pl.ds(t * H, H)], spins_out.at[t], sem.at[5]).start()
    for copy in copies[:-3]:
        copy.start()
    label[0] = jnp.max(small[0:1]).astype(jnp.int32)
    log[0] = jnp.max(small[1:2])
    beta[0] = jnp.max(small[2:3])
    for copy in copies[-3:]:
        copy.start()
    for copy in copies:
        copy.wait()
    pltpu.make_async_copy(spins_out, spins_out, sem.at[5]).wait()


def body(n, peers, total_rows, spins_in, noise, betas, labels, accept):
    _, rows, cols = spins_in.shape
    T, C = rows // H, cols // LANES
    blocks = rows // ROWS
    f32 = jnp.float32
    limit = VMEM_BYTES - 4 * (rows * cols + 2 * rows + 8 * LANES)
    hbm = pl.BlockSpec(memory_space=pltpu.HBM)
    vmem = pl.BlockSpec(memory_space=pltpu.VMEM)
    dma = pltpu.SemaphoreType.DMA
    accept = jnp.transpose(accept)
    labels = labels.reshape(1, 1)
    spins_in = spins_in.reshape(T, H, C, LANES).transpose(0, 2, 1, 3)
    noise = noise.reshape(SWEEPS, T, H, C, LANES).transpose(0, 1, 3, 2, 4)
    results = pl.pallas_call(
        functools.partial(kernel, n, peers, total_rows),
        out_shape=(
            pltpu.VMEM((C, rows, LANES), f32),
            pltpu.VMEM((1, rows), f32),
            pltpu.VMEM((1, rows), f32),
            pltpu.VMEM((8, LANES), f32),
        ),
        in_specs=[hbm] * 5,
        out_specs=(vmem,) * 4,
        scratch_shapes=[
            pltpu.VMEM((1 + SWEEPS, C, rows + 3 * PAD, LANES), f32),
            pltpu.VMEM((SWEEPS, T, C, H, LANES), jnp.bfloat16),
            *[pltpu.VMEM((C, rows // 2 + 2 * PAD, LANES), f32) for _ in range(STAGES)],
            pltpu.VMEM((C, rows, LANES), f32),
            pltpu.VMEM((rows, LANES), f32),
            pltpu.VMEM((2, rows, LANES), f32),
            pltpu.VMEM((2, 8, rows), f32),
            pltpu.VMEM((2, 8, rows), f32),
            pltpu.VMEM((8, LANES), f32),
            pltpu.VMEM((peers, 8, LANES), f32),
            pltpu.VMEM((8, LANES), f32),
            pltpu.VMEM((n, 8, LANES), f32),
            pltpu.SMEM(betas.shape, f32),
            pltpu.SMEM(labels.shape, jnp.int32),
            pltpu.SMEM(accept.shape, jnp.int32),
            dma((2,)),
            dma((SWEEPS, 2)),
            dma((2,)),
            dma((2,)),
            dma,
            dma((blocks // GATHER + 1,)),
            dma((2,)),
            dma((2,)),
            dma,
            dma,
            dma,
            dma,
            dma((3,)),
            pltpu.SemaphoreType.REGULAR((2,)),
        ],
        compiler_params=pltpu.CompilerParams(collective_id=0, has_side_effects=True, vmem_limit_bytes=limit),
        name="lattice_exchange",
    )(spins_in, noise, betas, labels, accept)
    out = pl.pallas_call(
        settle,
        out_shape=(
            jax.ShapeDtypeStruct(spins_in.shape, f32),
            jax.ShapeDtypeStruct((1, rows), f32),
            jax.ShapeDtypeStruct((1, rows), f32),
            jax.ShapeDtypeStruct((1,), jnp.int32),
            jax.ShapeDtypeStruct((1,), f32),
            jax.ShapeDtypeStruct((1,), f32),
        ),
        in_specs=[vmem] * 4,
        out_specs=(hbm,) * 6,
        scratch_shapes=[
            pltpu.SMEM((1,), jnp.int32),
            pltpu.SMEM((1,), f32),
            pltpu.SMEM((1,), f32),
            dma((6,)),
        ],
        compiler_params=pltpu.CompilerParams(vmem_limit_bytes=VMEM_BYTES // 2),
        name="settle",
    )(*results)
    spins = out[0].transpose(0, 2, 1, 3).reshape(1, rows, cols)
    return (spins, *out[1:])


def solution(mesh):
    n = mesh.shape["rep"]
    peers = mesh.shape["tile"]
    in_specs = (P("rep", "tile", None), P(None, "rep", "tile", None), P(), P("rep"), P(None, "rep"))
    out_specs = (P("rep", "tile", None), P("rep", "tile"), P("rep", "tile"), P("rep"), P("rep"), P("rep"))

    def run(spins_in, noise, betas, labels, accept):
        total_rows = spins_in.shape[1]
        step = jax.shard_map(
            functools.partial(body, n, peers, total_rows),
            mesh=mesh, in_specs=in_specs, out_specs=out_specs, check_vma=False,
        )
        return step(spins_in, noise, betas, labels, accept)

    return run
```

time: 61.8 us -> 57.4 us (0.929)
  the two profiles are of different devices: /device:TPU:0 before, /device:TPU:1 now
where the time goes in v1:
time: 57.4 us; the launch traced here: 56.8 us
  Pallas kernels  55.5 us (97%)
  between operations  1.29 us (2%)
    pallas_call x1, Pallas kernels, body(): pl.pallas_call(functools.partial(kernel, n, peers, total_rows), out_shape...  53.5 us
    pallas_call x1, Pallas kernels, body(): pl.pallas_call(settle, out_shape=(jax.ShapeDtypeStruct(spins_in.shape, f3...  2.04 us

profile of v1, /device:TPU:1, one launch (start us, length us, event | category | flops | bytes accessed | tf_op | source)
XLA Modules:
  0.0 56.8 jit_solution(6547662781456722332)
XLA Ops:
  1.3 53.5 %lattice_exchange.1 = (f32[32,256,128]{2,1,0:T(8,128)S(1)}, f32[1,256]{1,0:T(1,128)S(1)}, f32[1,256]{1,0:T(1,128)S(1)}, f32[8,128]{1,0:T(8,128)S(1)}) custom-call(f32[32,32,8,128]{3,2,1,0:T(8,128)} %bitcast.12, bf16[2,32,32,8,128]{4,3,2,1,0:T(8,128)(2,1)} %bitcast.13, f32[4]{0:T(128)} %betas_hbm.1, s32[1,1]{1,0:T(1,128)} %bitcast.11.labels_hbm, s32[1,2]{1,0:T(1,128)} %bitcast.14), custom_call_target="tpu_custom_call" | custom-call | tf_op jit(solution)/shard_map/lattice_exchange/pallas_call | solution.py:505
  54.8 2.0 %settle.1 = (f32[32,32,8,128]{3,2,1,0:T(8,128)}, f32[1,256]{1,0:T(1,128)}, f32[1,256]{1,0:T(1,128)}, s32[1]{0:T(128)}, f32[1]{0:T(128)}, /*index=5*/f32[1]{0:T(128)}) custom-call(f32[32,256,128]{2,1,0:T(8,128)S(1)} %get-tuple-element.16.spins, f32[1,256]{1,0:T(1,128)S(1)} %get-tuple-element.17.energy, f32[1,256]{1,0:T(1,128)S(1)} %get-tuple-element.18.margin, ...), custom_call_target="tpu_custom_call" | custom-call | tf_op jit(solution)/shard_map/settle/pallas_call | solution.py:549

commit v2 on v1

--- a/solution.py
+++ b/solution.py
@@ -13,10 +13,10 @@
 LANES = 128
 ROWS = 2 * H
 PAD = H
-EARLY = 9
+EARLY = 12
 HALO = 6
-PARTS = 4
 SOON = 6
+NEXT = 12
 GATHER = 4
 VMEM_BYTES = 60 * 1024 * 1024
 MESH = pl.DeviceIdType.MESH
@@ -43,7 +43,7 @@
     far = lax.rem(me + 2 + (n - 4) * odd, n)
     onward = lax.rem(me + n - 2 + 4 * odd, n)
 
-    part = half // PARTS
+    part = half // 2
     member = lax.rem((me + 1) // 2, 2)
     core = lax.rem(tile, 2)
     Q = (Q0, Q1, Q2, Q3)
@@ -54,12 +54,19 @@
         )
 
     def load_noise(w, start, stop, k):
-        return pltpu.make_async_copy(noise_ref.at[w, start:stop], NB.at[w, start:stop], n_sem.at[w, k])
-
-    def loaded(start, stop, k):
-        pltpu.make_async_copy(spins_ref.at[start:stop], spins_ref.at[start:stop], s_sem.at[k]).wait()
+        return pltpu.make_async_copy(noise_ref.at[w, start:stop], NB.at[w, start:stop], n_sem.at[k])
+
+    def load(start, stop, k):
         for w in range(SWEEPS):
-            load_noise(w, start, stop, k).wait()
+            load_noise(w, start, stop, k).start()
+
+        @pl.loop(start, stop)
+        def _(t):
+            load_spins(t, k).start()
+
+    def loaded(count, k):
+        for ref, sem in ((spins_ref.at[:count], s_sem), (noise_ref.at[:, :count], n_sem)):
+            pltpu.make_async_copy(ref, ref, sem.at[k]).wait()
 
     small = [
         pltpu.make_async_copy(src, dst, i_sem.at[k])
@@ -71,8 +78,8 @@
         copy.start()
 
     for w in range(SWEEPS):
-        load_noise(w, 0, SOON, 0).start()
-    for t in range(SOON):
+        load_noise(w, 1, SOON, 0).start()
+    for t in range(1, SOON):
         load_spins(t, 0).start()
 
     barrier = pltpu.get_barrier_semaphore()
@@ -97,11 +104,18 @@
         for side, (start, slot, dev) in enumerate(((rows, 0, nxt), (PAD, PAD + rows, prv)))
     ]
 
+    groups = blocks // GATHER
+    last_group = groups + 2
+
     def bulk(q, b, start, width):
         dest = lax.rem(me + (n - 2 + odd if q == 0 else 1 + odd), n)
         slot = 1 - odd if q == 0 else odd
         where = pl.ds(pl.multiple_of(b * ROWS, ROWS), ROWS)
-        group = (b // GATHER) if not isinstance(b, int) or b else blocks // GATHER
+        group = b // GATHER
+        if isinstance(b, int) and b == 0:
+            group = groups + slot
+        elif isinstance(b, int) and b == blocks - 1:
+            group = last_group
         return pltpu.make_async_remote_copy(
             X.at[pl.ds(q * half + start, width), where], R.at[pl.ds(slot * half + start, width), where],
             bs_sem, br_sem.at[group],
@@ -112,10 +126,10 @@
         for q in range(2):
             bulk(q, b, start, width).start()
 
-    def gathered(start, stop, group):
+    def gathered(start, stop, group, first=0, last=C):
         where = slice(start * ROWS, stop * ROWS)
         pltpu.make_async_remote_copy(
-            X.at[:, where], R.at[:, where], bs_sem, br_sem.at[group],
+            X.at[first:last, where], R.at[first:last, where], bs_sem, br_sem.at[group],
             device_id={"rep": near}, device_id_type=MESH,
         ).wait_recv()
 
@@ -211,14 +225,7 @@
     def _():
         forward()
 
-    loaded(0, SOON, 0)
-
-    for w in range(SWEEPS):
-        load_noise(w, SOON, T, 1).start()
-
-    @pl.loop(SOON, T)
-    def _(t):
-        load_spins(t, 1).start()
+    loaded(SOON - 1, 0)
 
     for copy in small:
         copy.wait()
@@ -233,7 +240,7 @@
             start, stop = low(reach), high(reach)
             spans.append([[(index + q * half + i) % C for i in range(start, stop)] for q in range(2)])
         for cs in spans[0]:
-            for t in range(SOON - 1):
+            for t in range(1, SOON - 1):
                 convert(t, cs)
         for k in range(STAGES):
             for cs in spans[k]:
@@ -253,16 +260,23 @@
         pl.semaphore_wait(go_sem.at[0], 2)
 
     send(1, 0, part)
+    load(SOON, NEXT, 1)
+    load(NEXT, T, 2)
     opening(lambda reach: reach, lambda reach: half - part + reach, part)
     send(1, part, half - part)
+    load(0, 1, 2)
     bonds(1)
-    loaded(SOON, T, 1)
+    loaded(NEXT - SOON, 1)
 
     @pl.loop(2, blocks + 1)
     def _(s):
         final = s // blocks
         middle = 1 - final
 
+        @pl.when(2 * s + 2 == NEXT)
+        def _():
+            loaded(T + 1 - NEXT, 2)
+
         @pl.when(s < blocks - 1)
         def _():
             convert(2 * s + 1)
@@ -271,6 +285,7 @@
         @pl.when(s == HALO)
         def _():
             convert(T - 1)
+            convert(0)
 
             @pl.when(member == 1)
             def _():
@@ -291,11 +306,12 @@
 
         b = middle * s
         finish(b)
-        bonds(b)
 
         @pl.when(s <= EARLY)
         def _():
             send(s)
+
+        bonds(b)
 
         @pl.when(s == HALO)
         def _():
@@ -350,39 +366,48 @@
     def _(d):
         ladder_copy(d).start()
 
-    @pl.loop(EARLY + 1, blocks)
+    @pl.loop(EARLY + 1, blocks - 1)
     def _(b):
         send(b)
 
+    def close():
+        send(blocks - 1)
+        send(0)
+
     @pl.when(core == 0)
     def _():
-        send(0)
-
-    def margins(b):
+        close()
+
+    def margins(b, wanted=(0, 1)):
         for g in range(2):
             where = pl.ds(pl.multiple_of(b * ROWS + g * H, H), H)
             totals = [jnp.zeros((H, LANES), jnp.float32) for _ in range(2)]
             for c in range(half):
-                own, one, two = X[odd * half + c, where, :], R[c, where, :], R[half + c, where, :]
-                totals[0] = totals[0] + own * one
-                totals[1] = totals[1] + one * two
-            for q in range(2):
+                one = R[c, where, :]
+                if 0 in wanted:
+                    totals[0] = totals[0] + X[odd * half + c, where, :] * one
+                if 1 in wanted:
+                    totals[1] = totals[1] + one * R[half + c, where, :]
+            for q in wanted:
                 MP[q, where, :] = totals[q]
 
-    def margin_sums(start, stop):
-        for q in range(2):
+    def margin_sums(start, stop, wanted=(0, 1)):
+        for q in wanted:
             sums = jnp.sum(MP[q, start:stop, :].T, axis=0, keepdims=True) * (1.0 / cols)
             MS[q, :, start:stop] = jnp.broadcast_to(sums, (8, stop - start))
 
     def collect(group):
-        start, stop = max(1, group * GATHER), (group + 1) * GATHER
+        start, stop = max(1, group * GATHER), min((group + 1) * GATHER, blocks - 1)
         gathered(start, stop, group)
+        if group == groups - 1:
+            @pl.when(core == 1)
+            def _():
+                close()
 
         @pl.loop(start, stop)
         def _(b):
             margins(b)
 
-    groups = blocks // GATHER
     for group in range(groups // 2):
         collect(group)
 
@@ -427,14 +452,9 @@
     for group in range(groups // 2, groups):
         collect(group)
 
-    @pl.when(core == 1)
-    def _():
-        send(0)
-
+    gathered(blocks - 1, blocks, last_group)
+    margins(blocks - 1)
     margin_sums(rows // 2, rows)
-    gathered(0, 1, groups)
-    margins(0)
-    margin_sums(0, rows // 2)
 
     home = pltpu.make_async_remote_copy(
         MS.at[1 - odd], MR.at[0], ms_sem.at[0], mr_sem.at[0], device_id={"rep": near}, device_id_type=MESH
@@ -442,7 +462,21 @@
     away = pltpu.make_async_remote_copy(
         MS.at[1], MR.at[1], ms_sem.at[1], mr_sem.at[1], device_id={"rep": far}, device_id_type=MESH
     )
-    home.start()
+    gathered(0, 1, groups, 0, half)
+    margins(0, (0,))
+    margin_sums(0, rows // 2, (0,))
+
+    @pl.when(odd == 1)
+    def _():
+        home.start()
+
+    gathered(0, 1, groups + 1, half, C)
+    margins(0, (1,))
+    margin_sums(0, rows // 2, (1,))
+
+    @pl.when(odd == 0)
+    def _():
+        home.start()
 
     @pl.when(odd == 1)
     def _():
@@ -528,12 +562,12 @@
             pltpu.SMEM(betas.shape, f32),
             pltpu.SMEM(labels.shape, jnp.int32),
             pltpu.SMEM(accept.shape, jnp.int32),
-            dma((2,)),
-            dma((SWEEPS, 2)),
+            dma((3,)),
+            dma((3,)),
             dma((2,)),
             dma((2,)),
             dma,
-            dma((blocks // GATHER + 1,)),
+            dma((blocks // GATHER + 3,)),
             dma((2,)),
             dma((2,)),
             dma,

time: 57.4 us -> 55.3 us (0.963)
  Pallas kernels: 55.5 us -> 53.9 us
    pallas_call x1, Pallas kernels: 53.5 us -> 51.8 us  [body(): pl.pallas_call(functools.partial(kernel, n, peers, total_rows), out_shape...]
where the time goes in v2:
time: 55.3 us; the launch traced here: 55.1 us
  Pallas kernels  53.9 us (97%)
  between operations  1.29 us (2%)
    pallas_call x1, Pallas kernels, body(): pl.pallas_call(functools.partial(kernel, n, peers, total_rows), out_shape...  51.8 us
    pallas_call x1, Pallas kernels, body(): pl.pallas_call(settle, out_shape=(jax.ShapeDtypeStruct(spins_in.shape, f3...  2.04 us

profile of v2, /device:TPU:1, one launch (start us, length us, event | category | flops | bytes accessed | tf_op | source)
XLA Modules:
  0.0 55.1 jit_solution(1242632782785360030)
XLA Ops:
  1.3 51.8 %lattice_exchange.1 = (f32[32,256,128]{2,1,0:T(8,128)S(1)}, f32[1,256]{1,0:T(1,128)S(1)}, f32[1,256]{1,0:T(1,128)S(1)}, f32[8,128]{1,0:T(8,128)S(1)}) custom-call(f32[32,32,8,128]{3,2,1,0:T(8,128)} %bitcast.12, bf16[2,32,32,8,128]{4,3,2,1,0:T(8,128)(2,1)} %bitcast.13, f32[4]{0:T(128)} %betas_hbm.1, s32[1,1]{1,0:T(1,128)} %bitcast.11.labels_hbm, s32[1,2]{1,0:T(1,128)} %bitcast.14), custom_call_target="tpu_custom_call" | custom-call | tf_op jit(solution)/shard_map/lattice_exchange/pallas_call | solution.py:539
  53.1 2.0 %settle.1 = (f32[32,32,8,128]{3,2,1,0:T(8,128)}, f32[1,256]{1,0:T(1,128)}, f32[1,256]{1,0:T(1,128)}, s32[1]{0:T(128)}, f32[1]{0:T(128)}, /*index=5*/f32[1]{0:T(128)}) custom-call(f32[32,256,128]{2,1,0:T(8,128)S(1)} %get-tuple-element.16.spins, f32[1,256]{1,0:T(1,128)S(1)} %get-tuple-element.17.energy, f32[1,256]{1,0:T(1,128)S(1)} %get-tuple-element.18.margin, ...), custom_call_target="tpu_custom_call" | custom-call | tf_op jit(solution)/shard_map/settle/pallas_call | solution.py:583
